TPU v7x, 32 devices: a whole 2x2x4 slice. The times are simulated.
32 devices in a mesh: member: 4 (over x, core), region: 8 (over z, y).
Axes of the slice: x: 2, y: 2, z: 4, core: 2. Of those that a mesh axis runs over, the one named last changes fastest.
Arguments:
- ensemble: float32 [12, 16, 32, 512], P('member', 'region'), may hold values from -6 to 6
- obs_value: float32 [16, 32, 128], P(None, ('member', 'region')), may hold values from -6 to 6
- obs_error: float32 [16, 32, 128], P(None, ('member', 'region')), may hold values from 0.5 to 4
- obs_index: int32 [16, 32, 128], P(None, ('member', 'region')), may hold values from 0 to 511
- obs_count: int32 [16, 32], P(None, ('member', 'region')), may hold values from 1 to 128
Outputs:
- analysis: float32 [12, 16, 32, 512], P('member', 'region')
Inputs may be any that keep to these rules, and one draw needn't show every extreme that they name: `obs_index`: value v names field v // (256) (0 SST, 1 SSH) at cell v mod (256) of the block, cells row-major. `obs_count`: slots below a block's count are observations; the others are padding and carry no weight.
All inputs are finite; a program needn't handle non-finite values.
Results may differ from a plain program's by a relative error of at most 0.0001.
Values sent between devices are 32-bit elements; how exact they have to be, the bound alone decides.
A program may use at most 64 MiB of HBM per device.

v0:
```python
import math
import jax
import jax.numpy as jnp
from jax import lax
from jax.sharding import PartitionSpec as P

SIDE = 16
NS_ITERS = 6
LOC_SCALE = 12.0
INFLATION_FACTOR = 1.1


def padded_2(cells, sides, width):
    for axis, dim in sides:
        count = lax.axis_size(axis)
        ends = count - 1
        head = lax.slice_in_dim(cells, 0, width, axis=dim)
        tail = lax.slice_in_dim(cells, cells.shape[dim] - width, cells.shape[dim], axis=dim)
        cells = jnp.concatenate(
            [
                lax.ppermute(tail, axis, [(i, (i + 1) % count) for i in range(ends)]),
                cells,
                lax.ppermute(head, axis, [((i + 1) % count, i) for i in range(ends)]),
            ],
            axis=dim,
        )
    return cells


def batch_product(left, right):
    return jnp.einsum("...ij,...jk->...ik", left, right, precision=lax.Precision.HIGHEST)


def observe(ensemble, obs_value, obs_error, obs_index, obs_count):
    ens_mean = jnp.mean(ensemble, axis=0)
    anomaly = ensemble - ens_mean
    slot_index = lax.broadcasted_iota(jnp.int32, obs_index.shape, 2)
    live_slot = jnp.where(slot_index < obs_count[:, :, None], 1.0, 0.0).astype(jnp.float32)
    root_weight = jnp.sqrt(live_slot / obs_error)
    value_count = anomaly.shape[3]
    value_ids = lax.broadcasted_iota(jnp.int32, (1, 1, 1, value_count), 3)
    selector = jnp.where(obs_index[:, :, :, None] == value_ids, 1.0, 0.0).astype(jnp.float32)
    seen_anom = jnp.einsum("rcov,krcv->rcko", selector, anomaly, precision=lax.Precision.HIGHEST)
    seen_mean = jnp.einsum("rcov,rcv->rco", selector, ens_mean, precision=lax.Precision.HIGHEST)
    rescaled_values = root_weight[:, :, None] * seen_anom
    innovation = root_weight * (obs_value - seen_mean)
    cell_index = obs_index % (SIDE * SIDE)
    rowpos = (cell_index // SIDE).astype(jnp.float32)
    column_position = (cell_index % SIDE).astype(jnp.float32)
    stacked = jnp.concatenate(
        [rescaled_values, innovation[:, :, None], rowpos[:, :, None], column_position[:, :, None]],
        axis=2,
    )
    return (anomaly, ens_mean, stacked)


def analyze(anomaly, ens_mean, padded):
    ensemble_members = anomaly.shape[0]
    row_count = anomaly.shape[1]
    col_count = anomaly.shape[2]
    pieces = []
    for row_step in range(3):
        for col_step in range(3):
            pieces.append(padded[row_step : row_step + row_count, col_step : col_step + col_count])
    nearby = jnp.stack(pieces, axis=2)
    rescaled_values = nearby[:, :, :, :ensemble_members]
    innovation = nearby[:, :, :, ensemble_members]
    rowpos = nearby[:, :, :, ensemble_members + 1]
    column_position = nearby[:, :, :, ensemble_members + 2]
    offset_index = jnp.arange(9, dtype=jnp.int32)
    offset_row = (offset_index // 3 - 1).astype(jnp.float32) * SIDE
    offset_col = (offset_index % 3 - 1).astype(jnp.float32) * SIDE
    half_side = SIDE // 2
    point_index = jnp.arange(4, dtype=jnp.int32)
    center_row = (point_index // 2).astype(jnp.float32) * half_side + (half_side - 1) * 0.5
    center_col = (point_index % 2).astype(jnp.float32) * half_side + (half_side - 1) * 0.5
    row_gap = offset_row[:, None] + rowpos
    col_gap = offset_col[:, None] + column_position
    distance = (row_gap[:, :, None] - center_row[:, None, None]) ** 2 + (
        col_gap[:, :, None] - center_col[:, None, None]
    ) ** 2
    locality = jnp.exp(-distance / (2.0 * LOC_SCALE * LOC_SCALE))
    weighted = locality[:, :, :, :, None, :] * rescaled_values[:, :, None]
    gramian_total = jnp.einsum(
        "rcpnko,rcnjo->rcpkj", weighted, rescaled_values, precision=lax.Precision.HIGHEST
    )
    drive_vec = jnp.einsum(
        "rcpnko,rcno->rcpk", weighted, innovation, precision=lax.Precision.HIGHEST
    )
    identity_matrix = jnp.eye(ensemble_members, dtype=jnp.float32)
    precision_matrix = gramian_total + (ensemble_members - 1) / INFLATION_FACTOR * identity_matrix
    norm_scale = jnp.sqrt(jnp.sum(precision_matrix * precision_matrix, axis=(3, 4), keepdims=True))
    root_iter = precision_matrix / norm_scale
    inv_iter = jnp.broadcast_to(identity_matrix, precision_matrix.shape)
    for sweep_index in range(NS_ITERS):
        ns_step = 1.5 * identity_matrix - 0.5 * batch_product(inv_iter, root_iter)
        root_iter = batch_product(root_iter, ns_step)
        inv_iter = batch_product(ns_step, inv_iter)
    inv_root = inv_iter / jnp.sqrt(norm_scale)
    half_way = jnp.einsum("rcpkj,rcpj->rcpk", inv_root, drive_vec, precision=lax.Precision.HIGHEST)
    mean_w = jnp.einsum("rcpkj,rcpj->rcpk", inv_root, half_way, precision=lax.Precision.HIGHEST)
    weights = mean_w[..., :, None] + math.sqrt(ensemble_members - 1) * inv_root
    point_weights = weights.reshape(row_count, col_count, 2, 2, ensemble_members, ensemble_members)
    shaped = anomaly.reshape(ensemble_members, row_count, col_count, 2, 2, half_side, 2, half_side)
    updated = jnp.einsum(
        "jrcvaybx,rcabjk->krcvaybx", shaped, point_weights, precision=lax.Precision.HIGHEST
    )
    return ens_mean[None] + updated.reshape(anomaly.shape)


def local(ensemble, obs_value, obs_error, obs_index, obs_count):
    members_dev = ensemble.shape[0]
    rows_dev = ensemble.shape[1]
    values_len = ensemble.shape[3]
    member_count = lax.axis_size("member")
    region_count = lax.axis_size("region")
    arrived = lax.all_to_all(
        ensemble[None], ("member", "region"), split_axis=3, concat_axis=0, tiled=True
    )
    col_dev = arrived.shape[3]
    grouped = arrived.reshape(
        member_count, region_count, members_dev, rows_dev, col_dev, values_len
    )
    by_block = jnp.transpose(grouped, (0, 2, 1, 3, 4, 5)).reshape(
        member_count * members_dev, region_count * rows_dev, col_dev, values_len
    )
    anomaly, ens_mean, stacked = observe(by_block, obs_value, obs_error, obs_index, obs_count)
    with_halo = padded_2(stacked, ((("member", "region"), 1),), 1)
    padded = jnp.pad(with_halo, ((1, 1), (0, 0), (0, 0), (0, 0)))
    row_span = anomaly.shape[1] // 8

    def one_group(turn_index, result):
        first_row_index = turn_index * row_span
        part_anom = lax.dynamic_slice_in_dim(anomaly, first_row_index, row_span, 1)
        part_mean = lax.dynamic_slice_in_dim(ens_mean, first_row_index, row_span, 0)
        part_pad = lax.dynamic_slice_in_dim(padded, first_row_index, row_span + 2, 0)
        return lax.dynamic_update_slice_in_dim(
            result, analyze(part_anom, part_mean, part_pad), first_row_index, 1
        )

    result = lax.fori_loop(0, 8, one_group, jnp.zeros_like(anomaly))
    col_dev = result.shape[2]
    regrouped = result.reshape(
        member_count, members_dev, region_count, rows_dev, col_dev, values_len
    )
    outgoing = jnp.transpose(regrouped, (0, 2, 1, 3, 4, 5)).reshape(
        member_count * region_count, members_dev, rows_dev, col_dev, values_len
    )
    returned = lax.all_to_all(
        outgoing, ("member", "region"), split_axis=0, concat_axis=3, tiled=True
    )
    return returned[0]


def solution(mesh):
    return jax.shard_map(
        local,
        mesh=mesh,
        in_specs=(
            P("member", "region", None, None),
            P(None, ("member", "region"), None),
            P(None, ("member", "region"), None),
            P(None, ("member", "region"), None),
            P(None, ("member", "region")),
        ),
        out_specs=P("member", "region", None, None),
        check_vma=False,
    )
```

profile of v0, /device:TPU:0, one launch (start us, length us, event | category | flops | bytes accessed | tf_op | source)
XLA Modules:
  0.0 172.5 jit_solution(10879895825682611400)
XLA Ops:
  2.1 7.3 %all-to-all-start = ((f32[1,3,2,32,512]{4,2,1,0,3:T(2,128)}), f32[1,3,2,32,512]{4,2,1,0,3:T(2,128)S(1)}, u32[]{:S(2)}, u32[]{:S(2)}) async-start(f32[1,3,2,32,512]{4,2,1,0,3:T(2,128)} %bitcast.189), calls=%async_computation | async-start | bytes 786432 | tf_op jit(solution)/shard_map/all_to_all | solution.py:117
  9.4 13.4 %all-to-all-done = f32[1,3,2,32,512]{4,2,1,0,3:T(2,128)S(1)} async-done(((f32[1,3,2,32,512]{4,2,1,0,3:T(2,128)}), f32[1,3,2,32,512]{4,2,1,0,3:T(2,128)S(1)}, u32[]{:S(2)}, u32[]{:S(2)}) %all-to-all-start) | async-done | bytes 393248 | tf_op jit(solution)/shard_map/all_to_all | solution.py:117
  23.4 4.1 %fusion.36 = f32[16,1,128]{2,1,0:T(1,128)S(1)} fusion(f32[16,512,1]{1,2,0:T(1,128)S(1)} %reshape.524, s32[16,128]{1,0:T(8,128)S(1)} %bitcast.316), kind=kOutput, calls=%fused_computation.88 | convolution fusion | flops 14680064 | bytes 49152 | tf_op jit(solution)/shard_map/rcov,rcv->rco/dot_general | solution.py:44
  27.6 4.0 %fusion.49 = f32[16,1,12,128]{3,2,0,1:T(8,128)S(1)} fusion(s32[16,128]{1,0:T(8,128)S(1)} %bitcast.317, f32[12,16,512]{2,1,0:T(8,128)S(1)} %broadcast_subtract_fusion.1, f32[16,128]{1,0:T(8,128)S(1)} %get-tuple-element.195), kind=kOutput, calls=%fused_computation.100 | convolution fusion | flops 153116672 | bytes 507904 | tf_op jit(solution)/shard_map/rcov,krcv->rcko/dot_general | solution.py:43
  31.6 2.9 %collective-permute-start = (f32[16,1,15,128]{3,2,0,1:T(8,128)S(1)}, f32[16,1,15,128]{3,2,0,1:T(8,128)S(1)}, u32[]{:S(2)}, u32[]{:S(2)}) collective-permute-start(f32[16,1,15,128]{3,2,0,1:T(8,128)S(1)} %pad_maximum_fusion), channel_id=1, source_target_pairs={{0,1},{1,2},{2,3},{3,4},{4,5},{5,6},{6,7},{7,8},{8,9},{9,10},{10,1... | collective-permute-start | bytes 368648 | tf_op jit(solution)/shard_map/ppermute | solution.py:21
  37.5 5.5 %collective-permute-done.1 = f32[16,1,15,128]{3,2,0,1:T(8,128)S(1)} collective-permute-done((f32[16,1,15,128]{3,2,0,1:T(8,128)S(1)}, f32[16,1,15,128]{3,2,0,1:T(8,128)S(1)}, u32[]{:S(2)}, u32[]{:S(2)}) %collective-permute-start.1) | collective-permute-done | bytes 122912 | tf_op jit(solution)/shard_map/ppermute | solution.py:23
  43.2 109.6 %while.16 = (s32[]{:T(128)}, f32[12,16,1,512]{3,1,0,2:T(8,128)S(1)}, f32[16,1,512]{2,0,1:T(8,128)S(1)}, f32[18,3,15,128]{3,2,0,1:T(8,128)S(1)}, f32[12,16,1,512]...) while((s32[]{:T(128)}, ...), condition=%wide.region_3.4_spmd, body=%wide.region_1.3_spmd.sunk | while | flops 22196300 | bytes 2025700 | solution.py:141
  43.7 2.4 %convolution_bitcast_fusion.7 = f32[2,4,12,1]{2,3,1,0:T(1,128)S(1)} fusion(f32[2,9,12,128]{3,2,1,0:T(8,128)S(1)} %slice_bitcast_fusion.2, f32[2,4,9,128]{3,2,1,0:T(8,128)S(1)} %multiply_exponential_fusion.2, f32[2,9,128,1,1]{2,0,1,3,4:T(2,128)S(1)} %bitcast.308), kind=kOutput, calls=%fused_computation.17.clone.1 | convolution fusion | flops 1437696 | bytes 157056 | tf_op jit(solution)/shard_map/while/body/eval_jaxpr/rcpnko,rcno->rcpk/dot_general | solution.py:87
  52.2 2.1 %convolution_bitcast_fusion.9 = f32[12,2,1,2,2,8,2,8]{0,7,5,3,6,4,1,2:T(8,128)S(1)} fusion(f32[2,2,2,12,12,1,1]{4,3,6,5,2,1,0:T(8,128)S(1)} %bitcast.300, f32[12,2,2,2,8,2,8]{6,5,4,3,2,1,0:T(2,128)S(1)} %reshape.527), kind=kOutput, calls=%fused_computation.clone.1 | convolution fusion | flops 1769472 | bytes 102912 | tf_op jit(solution)/shard_map/while/body/eval_jaxpr/jrcvaybx,rcabjk->krcvaybx/dot_general | solution.py:105
  57.4 2.4 %convolution_bitcast_fusion.7 = f32[2,4,12,1]{2,3,1,0:T(1,128)S(1)} fusion(f32[2,9,12,128]{3,2,1,0:T(8,128)S(1)} %slice_bitcast_fusion.2, f32[2,4,9,128]{3,2,1,0:T(8,128)S(1)} %multiply_exponential_fusion.2, f32[2,9,128,1,1]{2,0,1,3,4:T(2,128)S(1)} %bitcast.308), kind=kOutput, calls=%fused_computation.17.clone.1 | convolution fusion | flops 1437696 | bytes 157056 | tf_op jit(solution)/shard_map/while/body/eval_jaxpr/rcpnko,rcno->rcpk/dot_general | solution.py:87
  65.9 2.1 %convolution_bitcast_fusion.9 = f32[12,2,1,2,2,8,2,8]{0,7,5,3,6,4,1,2:T(8,128)S(1)} fusion(f32[2,2,2,12,12,1,1]{4,3,6,5,2,1,0:T(8,128)S(1)} %bitcast.300, f32[12,2,2,2,8,2,8]{6,5,4,3,2,1,0:T(2,128)S(1)} %reshape.527), kind=kOutput, calls=%fused_computation.clone.1 | convolution fusion | flops 1769472 | bytes 102912 | tf_op jit(solution)/shard_map/while/body/eval_jaxpr/jrcvaybx,rcabjk->krcvaybx/dot_general | solution.py:105
  71.1 2.4 %convolution_bitcast_fusion.7 = f32[2,4,12,1]{2,3,1,0:T(1,128)S(1)} fusion(f32[2,9,12,128]{3,2,1,0:T(8,128)S(1)} %slice_bitcast_fusion.2, f32[2,4,9,128]{3,2,1,0:T(8,128)S(1)} %multiply_exponential_fusion.2, f32[2,9,128,1,1]{2,0,1,3,4:T(2,128)S(1)} %bitcast.308), kind=kOutput, calls=%fused_computation.17.clone.1 | convolution fusion | flops 1437696 | bytes 157056 | tf_op jit(solution)/shard_map/while/body/eval_jaxpr/rcpnko,rcno->rcpk/dot_general | solution.py:87
  79.6 2.1 %convolution_bitcast_fusion.9 = f32[12,2,1,2,2,8,2,8]{0,7,5,3,6,4,1,2:T(8,128)S(1)} fusion(f32[2,2,2,12,12,1,1]{4,3,6,5,2,1,0:T(8,128)S(1)} %bitcast.300, f32[12,2,2,2,8,2,8]{6,5,4,3,2,1,0:T(2,128)S(1)} %reshape.527), kind=kOutput, calls=%fused_computation.clone.1 | convolution fusion | flops 1769472 | bytes 102912 | tf_op jit(solution)/shard_map/while/body/eval_jaxpr/jrcvaybx,rcabjk->krcvaybx/dot_general | solution.py:105
  84.8 2.4 %convolution_bitcast_fusion.7 = f32[2,4,12,1]{2,3,1,0:T(1,128)S(1)} fusion(f32[2,9,12,128]{3,2,1,0:T(8,128)S(1)} %slice_bitcast_fusion.2, f32[2,4,9,128]{3,2,1,0:T(8,128)S(1)} %multiply_exponential_fusion.2, f32[2,9,128,1,1]{2,0,1,3,4:T(2,128)S(1)} %bitcast.308), kind=kOutput, calls=%fused_computation.17.clone.1 | convolution fusion | flops 1437696 | bytes 157056 | tf_op jit(solution)/shard_map/while/body/eval_jaxpr/rcpnko,rcno->rcpk/dot_general | solution.py:87
  93.3 2.1 %convolution_bitcast_fusion.9 = f32[12,2,1,2,2,8,2,8]{0,7,5,3,6,4,1,2:T(8,128)S(1)} fusion(f32[2,2,2,12,12,1,1]{4,3,6,5,2,1,0:T(8,128)S(1)} %bitcast.300, f32[12,2,2,2,8,2,8]{6,5,4,3,2,1,0:T(2,128)S(1)} %reshape.527), kind=kOutput, calls=%fused_computation.clone.1 | convolution fusion | flops 1769472 | bytes 102912 | tf_op jit(solution)/shard_map/while/body/eval_jaxpr/jrcvaybx,rcabjk->krcvaybx/dot_general | solution.py:105
  98.5 2.4 %convolution_bitcast_fusion.7 = f32[2,4,12,1]{2,3,1,0:T(1,128)S(1)} fusion(f32[2,9,12,128]{3,2,1,0:T(8,128)S(1)} %slice_bitcast_fusion.2, f32[2,4,9,128]{3,2,1,0:T(8,128)S(1)} %multiply_exponential_fusion.2, f32[2,9,128,1,1]{2,0,1,3,4:T(2,128)S(1)} %bitcast.308), kind=kOutput, calls=%fused_computation.17.clone.1 | convolution fusion | flops 1437696 | bytes 157056 | tf_op jit(solution)/shard_map/while/body/eval_jaxpr/rcpnko,rcno->rcpk/dot_general | solution.py:87
  107.0 2.1 %convolution_bitcast_fusion.9 = f32[12,2,1,2,2,8,2,8]{0,7,5,3,6,4,1,2:T(8,128)S(1)} fusion(f32[2,2,2,12,12,1,1]{4,3,6,5,2,1,0:T(8,128)S(1)} %bitcast.300, f32[12,2,2,2,8,2,8]{6,5,4,3,2,1,0:T(2,128)S(1)} %reshape.527), kind=kOutput, calls=%fused_computation.clone.1 | convolution fusion | flops 1769472 | bytes 102912 | tf_op jit(solution)/shard_map/while/body/eval_jaxpr/jrcvaybx,rcabjk->krcvaybx/dot_general | solution.py:105
  112.2 2.4 %convolution_bitcast_fusion.7 = f32[2,4,12,1]{2,3,1,0:T(1,128)S(1)} fusion(f32[2,9,12,128]{3,2,1,0:T(8,128)S(1)} %slice_bitcast_fusion.2, f32[2,4,9,128]{3,2,1,0:T(8,128)S(1)} %multiply_exponential_fusion.2, f32[2,9,128,1,1]{2,0,1,3,4:T(2,128)S(1)} %bitcast.308), kind=kOutput, calls=%fused_computation.17.clone.1 | convolution fusion | flops 1437696 | bytes 157056 | tf_op jit(solution)/shard_map/while/body/eval_jaxpr/rcpnko,rcno->rcpk/dot_general | solution.py:87
  120.7 2.1 %convolution_bitcast_fusion.9 = f32[12,2,1,2,2,8,2,8]{0,7,5,3,6,4,1,2:T(8,128)S(1)} fusion(f32[2,2,2,12,12,1,1]{4,3,6,5,2,1,0:T(8,128)S(1)} %bitcast.300, f32[12,2,2,2,8,2,8]{6,5,4,3,2,1,0:T(2,128)S(1)} %reshape.527), kind=kOutput, calls=%fused_computation.clone.1 | convolution fusion | flops 1769472 | bytes 102912 | tf_op jit(solution)/shard_map/while/body/eval_jaxpr/jrcvaybx,rcabjk->krcvaybx/dot_general | solution.py:105
  125.9 2.4 %convolution_bitcast_fusion.7 = f32[2,4,12,1]{2,3,1,0:T(1,128)S(1)} fusion(f32[2,9,12,128]{3,2,1,0:T(8,128)S(1)} %slice_bitcast_fusion.2, f32[2,4,9,128]{3,2,1,0:T(8,128)S(1)} %multiply_exponential_fusion.2, f32[2,9,128,1,1]{2,0,1,3,4:T(2,128)S(1)} %bitcast.308), kind=kOutput, calls=%fused_computation.17.clone.1 | convolution fusion | flops 1437696 | bytes 157056 | tf_op jit(solution)/shard_map/while/body/eval_jaxpr/rcpnko,rcno->rcpk/dot_general | solution.py:87
  134.4 2.1 %convolution_bitcast_fusion.9 = f32[12,2,1,2,2,8,2,8]{0,7,5,3,6,4,1,2:T(8,128)S(1)} fusion(f32[2,2,2,12,12,1,1]{4,3,6,5,2,1,0:T(8,128)S(1)} %bitcast.300, f32[12,2,2,2,8,2,8]{6,5,4,3,2,1,0:T(2,128)S(1)} %reshape.527), kind=kOutput, calls=%fused_computation.clone.1 | convolution fusion | flops 1769472 | bytes 102912 | tf_op jit(solution)/shard_map/while/body/eval_jaxpr/jrcvaybx,rcabjk->krcvaybx/dot_general | solution.py:105
  139.6 2.4 %convolution_bitcast_fusion.7 = f32[2,4,12,1]{2,3,1,0:T(1,128)S(1)} fusion(f32[2,9,12,128]{3,2,1,0:T(8,128)S(1)} %slice_bitcast_fusion.2, f32[2,4,9,128]{3,2,1,0:T(8,128)S(1)} %multiply_exponential_fusion.2, f32[2,9,128,1,1]{2,0,1,3,4:T(2,128)S(1)} %bitcast.308), kind=kOutput, calls=%fused_computation.17.clone.1 | convolution fusion | flops 1437696 | bytes 157056 | tf_op jit(solution)/shard_map/while/body/eval_jaxpr/rcpnko,rcno->rcpk/dot_general | solution.py:87
  148.1 2.1 %convolution_bitcast_fusion.9 = f32[12,2,1,2,2,8,2,8]{0,7,5,3,6,4,1,2:T(8,128)S(1)} fusion(f32[2,2,2,12,12,1,1]{4,3,6,5,2,1,0:T(8,128)S(1)} %bitcast.300, f32[12,2,2,2,8,2,8]{6,5,4,3,2,1,0:T(2,128)S(1)} %reshape.527), kind=kOutput, calls=%fused_computation.clone.1 | convolution fusion | flops 1769472 | bytes 102912 | tf_op jit(solution)/shard_map/while/body/eval_jaxpr/jrcvaybx,rcabjk->krcvaybx/dot_general | solution.py:105
  153.0 18.6 %all_to_all.30 = f32[32,3,2,1,512]{4,2,1,3,0:T(2,128)S(1)} all-to-all(f32[32,3,2,1,512]{4,2,1,3,0:T(2,128)S(1)} %bitcast.305), channel_id=1, replica_groups=mesh['member'=4,'region'=8] {'member','region'}, dimensions={0} | all-to-all | bytes 786432 | tf_op jit(solution)/shard_map/all_to_all | solution.py:149
  (429 shorter events, 77.9 us)
Async XLA Ops:
  0.0 9.4 %copy-start = (s32[16,1,128]{2,1,0:T(1,128)S(1)}, s32[16,1,128]{2,1,0:T(1,128)}, u32[]{:S(2)}) copy-start(s32[16,1,128]{2,1,0:T(1,128)} %param.10) | copy-start | bytes 24580
  2.1 20.8 %all-to-all-start = ((f32[1,3,2,32,512]{4,2,1,0,3:T(2,128)}), f32[1,3,2,32,512]{4,2,1,0,3:T(2,128)S(1)}, u32[]{:S(2)}, u32[]{:S(2)}) async-start(f32[1,3,2,32,512]{4,2,1,0,3:T(2,128)} %bitcast.189), calls=%async_computation | async-start | bytes 786432 | tf_op jit(solution)/shard_map/all_to_all | solution.py:117
  23.4 4.1 %copy-start.1 = (f32[16,1,128]{2,1,0:T(1,128)S(1)}, f32[16,1,128]{2,1,0:T(1,128)}, u32[]{:S(2)}) copy-start(f32[16,1,128]{2,1,0:T(1,128)} %param.9) | copy-start | bytes 24580
  23.4 4.1 %copy-start.2 = (f32[16,1,128]{2,1,0:T(1,128)S(1)}, f32[16,1,128]{2,1,0:T(1,128)}, u32[]{:S(2)}) copy-start(f32[16,1,128]{2,1,0:T(1,128)} %param.8) | copy-start | bytes 24580
  23.4 4.1 %copy-start.3 = (s32[16,1]{0,1:T(1,128)S(1)}, s32[16,1]{0,1:T(1,128)}, u32[]{:S(2)}) copy-start(s32[16,1]{0,1:T(1,128)} %param.11) | copy-start | bytes 196
  31.6 5.9 %collective-permute-start = (f32[16,1,15,128]{3,2,0,1:T(8,128)S(1)}, f32[16,1,15,128]{3,2,0,1:T(8,128)S(1)}, u32[]{:S(2)}, u32[]{:S(2)}) collective-permute-start(f32[16,1,15,128]{3,2,0,1:T(8,128)S(1)} %pad_maximum_fusion), channel_id=1, source_target_pairs={{0,1},{1,2},{2,3},{3,4},{4,5},{5,6},{6,7},{7,8},{8,9},{9,10},{10,1... | collective-permute-start | bytes 368648 | tf_op jit(solution)/shard_map/ppermute | solution.py:21
  34.5 8.5 %collective-permute-start.1 = (f32[16,1,15,128]{3,2,0,1:T(8,128)S(1)}, f32[16,1,15,128]{3,2,0,1:T(8,128)S(1)}, u32[]{:S(2)}, u32[]{:S(2)}) collective-permute-start(f32[16,1,15,128]{3,2,0,1:T(8,128)S(1)} %pad_maximum_fusion), channel_id=1, source_target_pairs={{1,0},{2,1},{3,2},{4,3},{5,4},{6,5},{7,6},{8,7},{9,8},{10,9},{11,1... | collective-permute-start | bytes 368648 | tf_op jit(solution)/shard_map/ppermute | solution.py:23
where the time goes:
time: 173 us; the launch traced here: 172 us
  matrix products  79.8 us (46%)
  local copies, waits for them, and re-layouts  35.4 us (20%)
  waiting for transfers between devices  20.1 us (12%)
  blocking collectives  18.6 us (11%)
  starting transfers between devices  11.7 us (7%)
  other arithmetic  3.63 us (2%)
  loops' own time  3.01 us (2%)
    dot_general x136, matrix products, batch_product(): jnp.einsum('...ij,...jk->...ik', left, right, precision=lax.Precision.HIG...  26.5 us
    dot_general x8, matrix products, analyze(): jnp.einsum('rcpnko,rcno->rcpk', weighted, innovation, precision=lax.Preci...  19 us
    all_to_all x1, blocking collectives, local(): lax.all_to_all(outgoing, ('member', 'region'), split_axis=0, concat_axis=...  18.6 us
    dot_general x8, matrix products, analyze(): jnp.einsum('jrcvaybx,rcabjk->krcvaybx', shaped, point_weights, precision=...  16.6 us
    all_to_all x1, waiting for transfers between devices, local(): lax.all_to_all(ensemble[None], ('member', 'region'), split_axis=3, concat...  13.4 us
    transpose x8, local copies, waits for them, and re-layouts, analyze(): jnp.einsum('jrcvaybx,rcabjk->krcvaybx', shaped, point_weights, precision=...  11.2 us
    another operation x8, local copies, waits for them, and re-layouts  9.76 us
    reshape x8, local copies, waits for them, and re-layouts, analyze(): return ens_mean[None] + updated.reshape(anomaly.shape)  9.01 us
  transfers between devices with their start and end apart: 3, of which 3 were waited for; matrix products, arithmetic and copies ran while one was open for 0% of the time, Pallas kernels for 0%

commit v1 on v0

--- a/solution.py
+++ b/solution.py
@@ -114,9 +114,10 @@
     values_len = ensemble.shape[3]
     member_count = lax.axis_size("member")
     region_count = lax.axis_size("region")
-    arrived = lax.all_to_all(
-        ensemble[None], ("member", "region"), split_axis=3, concat_axis=0, tiled=True
-    )
+    part = ensemble[None]
+    parts = jnp.split(part, lax.axis_size(("member", "region")), axis=3)
+    received = lax.all_to_all(jnp.stack(parts), ("member", "region"), 0, 0)
+    arrived = jnp.concatenate(received, axis=0)
     col_dev = arrived.shape[3]
     grouped = arrived.reshape(
         member_count, region_count, members_dev, rows_dev, col_dev, values_len

time: 173 us -> 220 us (1.27)
  local copies, waits for them, and re-layouts: 35.4 us -> 81.6 us
    unnamed x9 -> x39, local copies, waits for them, and re-layouts: 2.09 us -> 46.6 us
    another operation x8 -> x10, local copies, waits for them, and re-layouts: 9.76 us -> 11.5 us
where the time goes in v1:
time: 220 us; the launch traced here: 219 us
  local copies, waits for them, and re-layouts  81.6 us (37%)
  matrix products  79.8 us (36%)
  waiting for transfers between devices  20.4 us (9%)
  blocking collectives  18.6 us (8%)
  starting transfers between devices  11.7 us (5%)
  other arithmetic  3.72 us (2%)
  loops' own time  3.01 us (1%)
    unnamed x39, local copies, waits for them, and re-layouts  46.6 us
    dot_general x136, matrix products, batch_product(): jnp.einsum('...ij,...jk->...ik', left, right, precision=lax.Precision.HIG...  26.5 us
    dot_general x8, matrix products, analyze(): jnp.einsum('rcpnko,rcno->rcpk', weighted, innovation, precision=lax.Preci...  19 us
    all_to_all x1, blocking collectives, local(): lax.all_to_all(outgoing, ('member', 'region'), split_axis=0, concat_axis=...  18.6 us
    dot_general x8, matrix products, analyze(): jnp.einsum('jrcvaybx,rcabjk->krcvaybx', shaped, point_weights, precision=...  16.6 us
    all_to_all x1, waiting for transfers between devices, local(): received = lax.all_to_all(jnp.stack(parts), ('member', 'region'), 0, 0)  13.4 us
    transpose x8, local copies, waits for them, and re-layouts, analyze(): jnp.einsum('jrcvaybx,rcabjk->krcvaybx', shaped, point_weights, precision=...  11.2 us
    another operation x8, local copies, waits for them, and re-layouts  9.76 us
  transfers between devices with their start and end apart: 3, of which 3 were waited for; matrix products, arithmetic and copies ran while one was open for 0% of the time, Pallas kernels for 0%

profile of v1, /device:TPU:0, one launch (start us, length us, event | category | flops | bytes accessed | tf_op | source)
XLA Modules:
  0.0 219.0 jit_solution(8128146561989934853)
XLA Ops:
  48.1 7.3 %all-to-all-start = ((f32[32,1,3,2,1,512]{5,4,3,2,1,0:T(1,128)}), f32[32,1,3,2,1,512]{5,4,3,2,1,0:T(1,128)S(1)}, u32[]{:S(2)}, u32[]{:S(2)}) async-start(f32[32,1,3,2,1,512]{5,4,3,2,1,0:T(1,128)} %constant_dynamic-update-slice_fusion.9), calls=%async_computation | async-start | bytes 786432 | tf_op jit(solution)/shard_map/all_to_all | solution.py:119
  55.5 13.4 %all-to-all-done = f32[32,1,3,2,1,512]{5,4,3,2,1,0:T(1,128)S(1)} async-done(((f32[32,1,3,2,1,512]{5,4,3,2,1,0:T(1,128)}), f32[32,1,3,2,1,512]{5,4,3,2,1,0:T(1,128)S(1)}, u32[]{:S(2)}, u32[]{:S(2)}) %all-to-all-start) | async-done | bytes 393248 | tf_op jit(solution)/shard_map/all_to_all | solution.py:119
  70.0 4.1 %fusion.36 = f32[16,1,128]{2,1,0:T(1,128)S(1)} fusion(f32[16,512,1]{1,2,0:T(1,128)S(1)} %reshape.519, s32[16,128]{1,0:T(8,128)S(1)} %bitcast.470), kind=kOutput, calls=%fused_computation.88 | convolution fusion | flops 14680064 | bytes 49152 | tf_op jit(solution)/shard_map/rcov,rcv->rco/dot_general | solution.py:44
  74.2 4.0 %fusion.49 = f32[16,1,12,128]{3,2,0,1:T(8,128)S(1)} fusion(s32[16,128]{1,0:T(8,128)S(1)} %bitcast.471, f32[12,16,512]{2,1,0:T(8,128)S(1)} %broadcast_subtract_fusion.1, f32[16,128]{1,0:T(8,128)S(1)} %get-tuple-element.195), kind=kOutput, calls=%fused_computation.100 | convolution fusion | flops 153116672 | bytes 507904 | tf_op jit(solution)/shard_map/rcov,krcv->rcko/dot_general | solution.py:43
  78.2 2.9 %collective-permute-start = (f32[16,1,15,128]{3,2,0,1:T(8,128)S(1)}, f32[16,1,15,128]{3,2,0,1:T(8,128)S(1)}, u32[]{:S(2)}, u32[]{:S(2)}) collective-permute-start(f32[16,1,15,128]{3,2,0,1:T(8,128)S(1)} %pad_maximum_fusion), channel_id=1, source_target_pairs={{0,1},{1,2},{2,3},{3,4},{4,5},{5,6},{6,7},{7,8},{8,9},{9,10},{10,1... | collective-permute-start | bytes 368648 | tf_op jit(solution)/shard_map/ppermute | solution.py:21
  84.1 5.5 %collective-permute-done.1 = f32[16,1,15,128]{3,2,0,1:T(8,128)S(1)} collective-permute-done((f32[16,1,15,128]{3,2,0,1:T(8,128)S(1)}, f32[16,1,15,128]{3,2,0,1:T(8,128)S(1)}, u32[]{:S(2)}, u32[]{:S(2)}) %collective-permute-start.1) | collective-permute-done | bytes 122912 | tf_op jit(solution)/shard_map/ppermute | solution.py:23
  89.7 109.6 %while.16 = (s32[]{:T(128)}, f32[12,16,1,512]{3,1,0,2:T(8,128)S(1)}, f32[16,1,512]{2,0,1:T(8,128)S(1)}, f32[18,3,15,128]{3,2,0,1:T(8,128)S(1)}, f32[12,16,1,512]...) while((s32[]{:T(128)}, ...), condition=%wide.region_3.4_spmd, body=%wide.region_1.3_spmd.sunk | while | flops 22196300 | bytes 2025700 | solution.py:142
  90.3 2.4 %convolution_bitcast_fusion.7 = f32[2,4,12,1]{2,3,1,0:T(1,128)S(1)} fusion(f32[2,9,12,128]{3,2,1,0:T(8,128)S(1)} %slice_bitcast_fusion.34, f32[2,4,9,128]{3,2,1,0:T(8,128)S(1)} %multiply_exponential_fusion.2, f32[2,9,128,1,1]{2,0,1,3,4:T(2,128)S(1)} %bitcast.462), kind=kOutput, calls=%fused_computation.17.clone.1 | convolution fusion | flops 1437696 | bytes 157056 | tf_op jit(solution)/shard_map/while/body/eval_jaxpr/rcpnko,rcno->rcpk/dot_general | solution.py:87
  98.7 2.1 convolution_bitcast_fusion.9
  104.0 2.4 %convolution_bitcast_fusion.7 = f32[2,4,12,1]{2,3,1,0:T(1,128)S(1)} fusion(f32[2,9,12,128]{3,2,1,0:T(8,128)S(1)} %slice_bitcast_fusion.34, f32[2,4,9,128]{3,2,1,0:T(8,128)S(1)} %multiply_exponential_fusion.2, f32[2,9,128,1,1]{2,0,1,3,4:T(2,128)S(1)} %bitcast.462), kind=kOutput, calls=%fused_computation.17.clone.1 | convolution fusion | flops 1437696 | bytes 157056 | tf_op jit(solution)/shard_map/while/body/eval_jaxpr/rcpnko,rcno->rcpk/dot_general | solution.py:87
  112.4 2.1 convolution_bitcast_fusion.9
  117.7 2.4 %convolution_bitcast_fusion.7 = f32[2,4,12,1]{2,3,1,0:T(1,128)S(1)} fusion(f32[2,9,12,128]{3,2,1,0:T(8,128)S(1)} %slice_bitcast_fusion.34, f32[2,4,9,128]{3,2,1,0:T(8,128)S(1)} %multiply_exponential_fusion.2, f32[2,9,128,1,1]{2,0,1,3,4:T(2,128)S(1)} %bitcast.462), kind=kOutput, calls=%fused_computation.17.clone.1 | convolution fusion | flops 1437696 | bytes 157056 | tf_op jit(solution)/shard_map/while/body/eval_jaxpr/rcpnko,rcno->rcpk/dot_general | solution.py:87
  126.1 2.1 convolution_bitcast_fusion.9
  131.4 2.4 %convolution_bitcast_fusion.7 = f32[2,4,12,1]{2,3,1,0:T(1,128)S(1)} fusion(f32[2,9,12,128]{3,2,1,0:T(8,128)S(1)} %slice_bitcast_fusion.34, f32[2,4,9,128]{3,2,1,0:T(8,128)S(1)} %multiply_exponential_fusion.2, f32[2,9,128,1,1]{2,0,1,3,4:T(2,128)S(1)} %bitcast.462), kind=kOutput, calls=%fused_computation.17.clone.1 | convolution fusion | flops 1437696 | bytes 157056 | tf_op jit(solution)/shard_map/while/body/eval_jaxpr/rcpnko,rcno->rcpk/dot_general | solution.py:87
  139.8 2.1 convolution_bitcast_fusion.9
  145.1 2.4 %convolution_bitcast_fusion.7 = f32[2,4,12,1]{2,3,1,0:T(1,128)S(1)} fusion(f32[2,9,12,128]{3,2,1,0:T(8,128)S(1)} %slice_bitcast_fusion.34, f32[2,4,9,128]{3,2,1,0:T(8,128)S(1)} %multiply_exponential_fusion.2, f32[2,9,128,1,1]{2,0,1,3,4:T(2,128)S(1)} %bitcast.462), kind=kOutput, calls=%fused_computation.17.clone.1 | convolution fusion | flops 1437696 | bytes 157056 | tf_op jit(solution)/shard_map/while/body/eval_jaxpr/rcpnko,rcno->rcpk/dot_general | solution.py:87
  153.5 2.1 convolution_bitcast_fusion.9
  158.8 2.4 %convolution_bitcast_fusion.7 = f32[2,4,12,1]{2,3,1,0:T(1,128)S(1)} fusion(f32[2,9,12,128]{3,2,1,0:T(8,128)S(1)} %slice_bitcast_fusion.34, f32[2,4,9,128]{3,2,1,0:T(8,128)S(1)} %multiply_exponential_fusion.2, f32[2,9,128,1,1]{2,0,1,3,4:T(2,128)S(1)} %bitcast.462), kind=kOutput, calls=%fused_computation.17.clone.1 | convolution fusion | flops 1437696 | bytes 157056 | tf_op jit(solution)/shard_map/while/body/eval_jaxpr/rcpnko,rcno->rcpk/dot_general | solution.py:87
  167.2 2.1 convolution_bitcast_fusion.9
  172.5 2.4 %convolution_bitcast_fusion.7 = f32[2,4,12,1]{2,3,1,0:T(1,128)S(1)} fusion(f32[2,9,12,128]{3,2,1,0:T(8,128)S(1)} %slice_bitcast_fusion.34, f32[2,4,9,128]{3,2,1,0:T(8,128)S(1)} %multiply_exponential_fusion.2, f32[2,9,128,1,1]{2,0,1,3,4:T(2,128)S(1)} %bitcast.462), kind=kOutput, calls=%fused_computation.17.clone.1 | convolution fusion | flops 1437696 | bytes 157056 | tf_op jit(solution)/shard_map/while/body/eval_jaxpr/rcpnko,rcno->rcpk/dot_general | solution.py:87
  180.9 2.1 convolution_bitcast_fusion.9
  186.2 2.4 %convolution_bitcast_fusion.7 = f32[2,4,12,1]{2,3,1,0:T(1,128)S(1)} fusion(f32[2,9,12,128]{3,2,1,0:T(8,128)S(1)} %slice_bitcast_fusion.34, f32[2,4,9,128]{3,2,1,0:T(8,128)S(1)} %multiply_exponential_fusion.2, f32[2,9,128,1,1]{2,0,1,3,4:T(2,128)S(1)} %bitcast.462), kind=kOutput, calls=%fused_computation.17.clone.1 | convolution fusion | flops 1437696 | bytes 157056 | tf_op jit(solution)/shard_map/while/body/eval_jaxpr/rcpnko,rcno->rcpk/dot_general | solution.py:87
  194.6 2.1 convolution_bitcast_fusion.9
  199.6 18.6 %all_to_all.20 = f32[32,3,2,1,512]{4,2,1,3,0:T(2,128)S(1)} all-to-all(f32[32,3,2,1,512]{4,2,1,3,0:T(2,128)S(1)} %bitcast.427), channel_id=1, replica_groups=mesh['member'=4,'region'=8] {'member','region'}, dimensions={0} | all-to-all | bytes 786432 | tf_op jit(solution)/shard_map/all_to_all | solution.py:150
  (460 shorter events, 124.4 us)
Async XLA Ops:
  0.0 55.4 %copy-start = (s32[16,1,128]{2,1,0:T(1,128)S(1)}, s32[16,1,128]{2,1,0:T(1,128)}, u32[]{:S(2)}) copy-start(s32[16,1,128]{2,1,0:T(1,128)} %param.10) | copy-start | bytes 24580
  48.1 20.8 %all-to-all-start = ((f32[32,1,3,2,1,512]{5,4,3,2,1,0:T(1,128)}), f32[32,1,3,2,1,512]{5,4,3,2,1,0:T(1,128)S(1)}, u32[]{:S(2)}, u32[]{:S(2)}) async-start(f32[32,1,3,2,1,512]{5,4,3,2,1,0:T(1,128)} %constant_dynamic-update-slice_fusion.9), calls=%async_computation | async-start | bytes 786432 | tf_op jit(solution)/shard_map/all_to_all | solution.py:119
  70.0 4.1 %copy-start.1 = (f32[16,1,128]{2,1,0:T(1,128)S(1)}, f32[16,1,128]{2,1,0:T(1,128)}, u32[]{:S(2)}) copy-start(f32[16,1,128]{2,1,0:T(1,128)} %param.9) | copy-start | bytes 24580
  70.0 4.1 %copy-start.2 = (f32[16,1,128]{2,1,0:T(1,128)S(1)}, f32[16,1,128]{2,1,0:T(1,128)}, u32[]{:S(2)}) copy-start(f32[16,1,128]{2,1,0:T(1,128)} %param.8) | copy-start | bytes 24580
  70.0 4.1 %copy-start.3 = (s32[16,1]{0,1:T(1,128)S(1)}, s32[16,1]{0,1:T(1,128)}, u32[]{:S(2)}) copy-start(s32[16,1]{0,1:T(1,128)} %param.11) | copy-start | bytes 196
  78.2 5.9 %collective-permute-start = (f32[16,1,15,128]{3,2,0,1:T(8,128)S(1)}, f32[16,1,15,128]{3,2,0,1:T(8,128)S(1)}, u32[]{:S(2)}, u32[]{:S(2)}) collective-permute-start(f32[16,1,15,128]{3,2,0,1:T(8,128)S(1)} %pad_maximum_fusion), channel_id=1, source_target_pairs={{0,1},{1,2},{2,3},{3,4},{4,5},{5,6},{6,7},{7,8},{8,9},{9,10},{10,1... | collective-permute-start | bytes 368648 | tf_op jit(solution)/shard_map/ppermute | solution.py:21
  81.1 8.5 %collective-permute-start.1 = (f32[16,1,15,128]{3,2,0,1:T(8,128)S(1)}, f32[16,1,15,128]{3,2,0,1:T(8,128)S(1)}, u32[]{:S(2)}, u32[]{:S(2)}) collective-permute-start(f32[16,1,15,128]{3,2,0,1:T(8,128)S(1)} %pad_maximum_fusion), channel_id=1, source_target_pairs={{1,0},{2,1},{3,2},{4,3},{5,4},{6,5},{7,6},{8,7},{9,8},{10,9},{11,1... | collective-permute-start | bytes 368648 | tf_op jit(solution)/shard_map/ppermute | solution.py:23
